TPU v7x, 32 devices: a whole 2x2x4 slice. The times are simulated.
32 devices in a mesh: row: 8 (over z, y), col: 4 (over x, core).
Axes of the slice: x: 2, y: 2, z: 4, core: 2. Of those that a mesh axis runs over, the one named last changes fastest.
Arguments:
- moment: bfloat16 [2, 4096, 4096], P(None, 'row', 'col'), may hold values from -6 to 6
- second: float32 [2, 4096, 4096], P(None, 'row', 'col'), may hold values from 0.04 to 2
- left_old: bfloat16 [2, 4096, 4096], P(None, 'col', 'row'), may hold values from -0.09375 to 0.09375
- left_new: bfloat16 [2, 4096, 4096], P(None, 'col', 'row'), may hold values from -0.09375 to 0.09375
- right_old: bfloat16 [4096, 4096], P('row', 'col'), may hold values from -0.09375 to 0.09375
- right_new: bfloat16 [4096, 4096], P('row', 'col'), may hold values from -0.09375 to 0.09375
Outputs:
- moment_new: bfloat16 [2, 4096, 4096], P(None, 'row', 'col')
- direction: bfloat16 [2, 4096, 4096], P(None, 'row', 'col')
All inputs are finite; a program needn't handle non-finite values.
Results may differ from a plain program's by a relative error of at most 0.03.
Values may be sent and summed in bfloat16 or wider, within the bound.
A program may use at most 128 MiB of HBM per device.

v0:
```python
import jax
import jax.numpy as jnp
from jax import lax
from jax.sharding import PartitionSpec as P


def fold_stacked(left_panel, incoming):
    return jnp.einsum("bij,bjk->bik", left_panel, incoming, preferred_element_type=jnp.float32)


def fold_right(right_panel, incoming):
    return jnp.einsum("bik,qk->biq", incoming, right_panel, preferred_element_type=jnp.float32)


def local(moment, second, left_old, left_new, right_old, right_new):
    old_right_rows = lax.all_gather(right_old, "col", axis=1, tiled=True)
    right_terms = jnp.dot(right_new.T, old_right_rows, preferred_element_type=jnp.float32)
    right_panel = lax.psum(right_terms.astype(jnp.bfloat16), "row")
    old_rows = lax.all_gather(left_old, "row", axis=2, tiled=True)
    left_terms = jnp.einsum("bwi,bwj->bij", left_new, old_rows, preferred_element_type=jnp.float32)
    left_panel = lax.psum(left_terms.astype(jnp.bfloat16), "col")
    summed = fold_stacked(left_panel, lax.all_gather(moment, "row", axis=1, tiled=True))
    rotated = summed.astype(jnp.bfloat16)
    result = fold_right(right_panel, lax.all_gather(rotated, "col", axis=2, tiled=True))
    moment_new = result.astype(jnp.bfloat16)
    direction = (moment_new.astype(jnp.float32) / (jnp.sqrt(second) + 1e-08)).astype(jnp.bfloat16)
    return (moment_new, direction)


def solution(mesh):
    return jax.shard_map(
        local,
        mesh=mesh,
        in_specs=(
            P(None, "row", "col"),
            P(None, "row", "col"),
            P(None, "col", "row"),
            P(None, "col", "row"),
            P("row", "col"),
            P("row", "col"),
        ),
        out_specs=(P(None, "row", "col"), P(None, "row", "col")),
        check_vma=False,
    )
```

profile of v0, /device:TPU:0, one launch (start us, length us, event | category | flops | bytes accessed | tf_op | source)
XLA Modules:
  0.0 1013.9 jit_solution(3959504421610417472)
XLA Ops:
  7.2 0.0 copy-start
  7.2 0.0 all-gather.5.cloned.1.call-start
  7.2 0.7 all-gather.5.cloned.1.call-update
  7.9 0.0 all-gather.11.cloned.1.call-start
  8.0 0.7 all-gather.11.cloned.1.call-update
  8.7 0.0 all-gather.7.cloned.1.call-start
  8.7 0.7 all-gather.7.cloned.1.call-update
  9.4 0.0 all-reduce.3.cloned.1.call-start
  9.4 230.6 %all-gather.5.cloned.1.call-done = bf16[2,1024,4096]{2,1,0:T(8,128)(2,1)} async-done(((bf16[2,1024,512]{2,1,0:T(8,128)(2,1)}), bf16[2,1024,4096]{2,1,0:T(8,128)(2,1)}) %all-gather.5.cloned.1.call-update) | async-done | bytes 16777232 | tf_op jit(solution)/shard_map/all_gather | solution.py:19
  240.1 0.0 copy-done
  240.1 17.1 %convolution_convert_fusion.1 = bf16[2,512,4096]{2,1,0:T(8,128)(2,1)} fusion(bf16[2,1024,512]{2,1,0:T(8,128)(2,1)S(1)} %copy-done, bf16[2,1024,4096]{2,1,0:T(8,128)(2,1)} %all-gather.5.cloned.1.call-done), kind=kOutput, calls=%fused_computation.3 | convolution fusion | flops 8594128896 | bytes 27262976 | tf_op jit(solution)/shard_map/bwi,bwj->bij/dot_general | solution.py:20
  257.2 0.0 copy-start.2
  257.2 0.0 all-reduce.3.cloned.1.call-update
  257.2 0.0 all-reduce.5.cloned.1.call-start
  257.2 17.1 %all-gather.11.cloned.1.call-done = bf16[512,4096]{1,0:T(8,128)(2,1)} async-done(((bf16[512,1024]{1,0:T(8,128)(2,1)}), bf16[512,4096]{1,0:T(8,128)(2,1)}) %all-gather.11.cloned.1.call-update) | async-done | bytes 4194320 | tf_op jit(solution)/shard_map/all_gather | solution.py:16
  274.3 0.0 copy-done.2
  274.3 8.9 convolution_convert_fusion
  283.3 0.0 all-reduce.5.cloned.1.call-update
  283.3 0.2 all-gather.9.cloned.1.call-start
  283.5 220.3 %all-gather.7.cloned.1.call-done = bf16[2,4096,1024]{2,1,0:T(8,128)(2,1)} async-done(((bf16[2,512,1024]{2,1,0:T(8,128)(2,1)}), bf16[2,4096,1024]{2,1,0:T(8,128)(2,1)}) %all-gather.7.cloned.1.call-update) | async-done | bytes 16777232 | tf_op jit(solution)/shard_map/all_gather | solution.py:22
  503.8 153.4 %all-reduce.3.cloned.1.call-done = bf16[2,512,4096]{2,1,0:T(8,128)(2,1)} async-done(((bf16[2,512,4096]{2,1,0:T(8,128)(2,1)}), bf16[2,512,4096]{2,1,0:T(8,128)(2,1)}) %all-reduce.3.cloned.1.call-update) | async-done | bytes 8388624 | tf_op jit(solution)/shard_map/psum | solution.py:21
  657.2 15.8 %convolution_convert_fusion.2 = bf16[2,512,1024]{2,1,0:T(8,128)(2,1)} fusion(bf16[2,512,4096]{2,1,0:T(8,128)(2,1)} %all-reduce.3.cloned.1.call-done, bf16[2,4096,1024]{2,1,0:T(8,128)(2,1)} %all-gather.7.cloned.1.call-done), kind=kOutput, calls=%fused_computation.6 | convolution fusion | flops 8590983168 | bytes 27262976 | tf_op jit(solution)/shard_map/bij,bjk->bik/dot_general | solution.py:8
  673.0 0.0 all-gather.9.cloned.1.call-update
  673.0 258.1 %all-reduce.5.cloned.1.call-done = bf16[1024,4096]{1,0:T(8,128)(2,1)} async-done(((bf16[1024,4096]{1,0:T(8,128)(2,1)}), bf16[1024,4096]{1,0:T(8,128)(2,1)}) %all-reduce.5.cloned.1.call-update) | async-done | bytes 8388624 | tf_op jit(solution)/shard_map/psum | solution.py:18
  931.1 59.4 %all-gather.9.cloned.1.call-done = bf16[2,512,4096]{2,1,0:T(8,128)(2,1)} async-done(((bf16[2,512,1024]{2,1,0:T(8,128)(2,1)}), bf16[2,512,4096]{2,1,0:T(8,128)(2,1)}) %all-gather.9.cloned.1.call-update) | async-done | bytes 8388624 | tf_op jit(solution)/shard_map/all_gather | solution.py:24
  990.5 0.0 copy-start.1
  990.5 16.6 %divide_convert_fusion = (bf16[2,512,1024]{2,1,0:T(8,128)(2,1)}, bf16[2,512,1024]{2,1,0:T(8,128)(2,1)}) fusion(f32[2,512,1024]{2,1,0:T(8,128)} %param.7, bf16[2,512,4096]{2,1,0:T(8,128)(2,1)} %all-gather.9.cloned.1.call-done, bf16[1024,4096]{1,0:T(8,128)(2,1)} %all-reduce.5.cloned.1.call-done), kind=kOutput, calls=%fused_computation.4 | convolution fusion | flops 8595177472 | bytes 25165824 | tf_op jit(solution)/shard_map/bik,qk->biq/dot_general | solution.py:12
  1007.1 0.0 copy-done.1
Async XLA Ops:
  7.2 232.9 %copy-start = (bf16[2,1024,512]{2,1,0:T(8,128)(2,1)S(1)}, bf16[2,1024,512]{2,1,0:T(8,128)(2,1)}, u32[]{:S(2)}) copy-start(bf16[2,1024,512]{2,1,0:T(8,128)(2,1)} %param.9) | copy-start | bytes 6291460
  7.2 232.9 %all-gather.5.cloned.1.call-start = ((), (), s32[]{:S(2)}) async-start(), calls=%async_computation | async-start | bytes 18874368 | tf_op jit(solution)/shard_map/all_gather | solution.py:19
  7.9 266.4 %all-gather.11.cloned.1.call-start = ((), (), s32[]{:S(2)}) async-start(), calls=%async_computation.4 | async-start | bytes 5242880 | tf_op jit(solution)/shard_map/all_gather | solution.py:16
  8.7 495.1 %all-gather.7.cloned.1.call-start = ((), (), s32[]{:S(2)}) async-start(), calls=%async_computation.2 | async-start | bytes 18874368 | tf_op jit(solution)/shard_map/all_gather | solution.py:22
  9.4 647.8 %all-reduce.3.cloned.1.call-start = ((), (), s32[]{:S(2)}) async-start(), calls=%async_computation.1 | async-start | bytes 16777216 | tf_op jit(solution)/shard_map/psum | solution.py:21
  257.2 17.2 %copy-start.2 = (bf16[512,1024]{1,0:T(8,128)(2,1)S(1)}, bf16[512,1024]{1,0:T(8,128)(2,1)}, u32[]{:S(2)}) copy-start(bf16[512,1024]{1,0:T(8,128)(2,1)} %param.11) | copy-start | bytes 3145732
  257.2 673.9 %all-reduce.5.cloned.1.call-start = ((), (), s32[]{:S(2)}) async-start(), calls=%async_computation.5 | async-start | bytes 16777216 | tf_op jit(solution)/shard_map/psum | solution.py:18
  283.3 707.2 %all-gather.9.cloned.1.call-start = ((), (), s32[]{:S(2)}) async-start(), calls=%async_computation.3 | async-start | bytes 10485760 | tf_op jit(solution)/shard_map/all_gather | solution.py:24
  990.5 16.6 %copy-start.1 = (bf16[2,1024,512]{2,1,0:T(8,128)(2,1)S(1)}, bf16[2,1024,512]{2,1,0:T(8,128)(2,1)}, u32[]{:S(2)}) copy-start(bf16[2,1024,512]{2,1,0:T(8,128)(2,1)} %param.9) | copy-start | bytes 6291460
Sparse Core Ops, SparseCore 0:
  10.0 230.0 all-gather.4
  241.6 32.6 all-gather.10
  276.5 227.2 all-gather.6
  506.1 151.0 all-reduce.2
  660.9 270.1 all-reduce.4
  933.1 57.3 all-gather.8
where the time goes:
time: 1010 us
  waiting for transfers between devices  941 us (93%)
  matrix products  58.4 us (6%)
  between operations  14.1 us (1%)
    psum x1, waiting for transfers between devices, local(): right_panel = lax.psum(right_terms.astype(jnp.bfloat16), 'row')  258 us
    all_gather x1, waiting for transfers between devices, local(): old_rows = lax.all_gather(left_old, 'row', axis=2, tiled=True)  231 us
    all_gather x1, waiting for transfers between devices, local(): lax.all_gather(moment, 'row', axis=1, tiled=True)  220 us
    psum x1, waiting for transfers between devices, local(): left_panel = lax.psum(left_terms.astype(jnp.bfloat16), 'col')  153 us
    all_gather x1, waiting for transfers between devices, local(): lax.all_gather(rotated, 'col', axis=2, tiled=True)  59.4 us
  transfers between devices with their start and end apart: 6, of which 6 were waited for; matrix products, arithmetic and copies ran while one was open for 4% of the time, Pallas kernels for 0%

commit v1 on v0

--- a/solution.py
+++ b/solution.py
@@ -2,6 +2,11 @@
 import jax.numpy as jnp
 from jax import lax
 from jax.sharding import PartitionSpec as P
+
+
+def gathered_along(array, mesh_axis, dim):
+    pieces = lax.all_gather(array, mesh_axis)
+    return jnp.concatenate(pieces, axis=dim)
 
 
 def fold_stacked(left_panel, incoming):
@@ -19,7 +24,7 @@
     old_rows = lax.all_gather(left_old, "row", axis=2, tiled=True)
     left_terms = jnp.einsum("bwi,bwj->bij", left_new, old_rows, preferred_element_type=jnp.float32)
     left_panel = lax.psum(left_terms.astype(jnp.bfloat16), "col")
-    summed = fold_stacked(left_panel, lax.all_gather(moment, "row", axis=1, tiled=True))
+    summed = fold_stacked(left_panel, gathered_along(moment, "row", 1))
     rotated = summed.astype(jnp.bfloat16)
     result = fold_right(right_panel, lax.all_gather(rotated, "col", axis=2, tiled=True))
     moment_new = result.astype(jnp.bfloat16)

time: 1010 us -> 1010 us (level)
  waiting for transfers between devices: 941 us -> 927 us
  local copies, waits for them, and re-layouts: 0.02 us -> 14 us
    psum x1, waiting for transfers between devices: 153 us -> 139 us  [local(): left_panel = lax.psum(left_terms.astype(jnp.bfloat16), 'col')]
    reshape x0 -> x1, local copies, waits for them, and re-layouts: none -> 13.9 us  [gathered_along(): return jnp.concatenate(pieces, axis=dim)]
  transfers between devices with their start and end apart: 6 -> 6, of which waited for: 6 -> 6; matrix products, arithmetic and copies ran while one was open for 4% -> 5% of each run, Pallas kernels for 0% -> 0%
where the time goes in v1:
time: 1010 us
  waiting for transfers between devices  927 us (92%)
  matrix products  58.4 us (6%)
  between operations  14.1 us (1%)
  local copies, waits for them, and re-layouts  14 us (1%)
    psum x1, waiting for transfers between devices, local(): right_panel = lax.psum(right_terms.astype(jnp.bfloat16), 'row')  258 us
    all_gather x1, waiting for transfers between devices, local(): old_rows = lax.all_gather(left_old, 'row', axis=2, tiled=True)  231 us
    all_gather x1, waiting for transfers between devices, gathered_along(): pieces = lax.all_gather(array, mesh_axis)  220 us
    psum x1, waiting for transfers between devices, local(): left_panel = lax.psum(left_terms.astype(jnp.bfloat16), 'col')  139 us
    all_gather x1, waiting for transfers between devices, local(): lax.all_gather(rotated, 'col', axis=2, tiled=True)  59.4 us
  transfers between devices with their start and end apart: 6, of which 6 were waited for; matrix products, arithmetic and copies ran while one was open for 5% of the time, Pallas kernels for 0%

profile of v1, /device:TPU:0, one launch (start us, length us, event | category | flops | bytes accessed | tf_op | source)
XLA Modules:
  0.0 1013.9 jit_solution(15849557869698540945)
XLA Ops:
  7.2 0.0 copy-start
  7.2 0.0 all-gather.6.cloned.1.call-start
  7.2 0.7 all-gather.6.cloned.1.call-update
  7.9 0.0 all-gather.10.cloned.1.call-start
  8.0 0.7 all-gather.10.cloned.1.call-update
  8.7 0.0 all-gather.12.cloned.1.call-start
  8.7 0.7 all-gather.12.cloned.1.call-update
  9.4 0.0 all-reduce.3.cloned.1.call-start
  9.4 230.6 %all-gather.6.cloned.1.call-done = bf16[2,1024,4096]{2,1,0:T(8,128)(2,1)} async-done(((bf16[2,1024,512]{2,1,0:T(8,128)(2,1)}), bf16[2,1024,4096]{2,1,0:T(8,128)(2,1)}) %all-gather.6.cloned.1.call-update) | async-done | bytes 16777232 | tf_op jit(solution)/shard_map/all_gather | solution.py:24
  240.1 0.0 copy-done
  240.1 17.1 %convolution_convert_fusion.1 = bf16[2,512,4096]{2,1,0:T(8,128)(2,1)} fusion(bf16[2,1024,512]{2,1,0:T(8,128)(2,1)S(1)} %copy-done, bf16[2,1024,4096]{2,1,0:T(8,128)(2,1)} %all-gather.6.cloned.1.call-done), kind=kOutput, calls=%fused_computation.3 | convolution fusion | flops 8594128896 | bytes 27262976 | tf_op jit(solution)/shard_map/bwi,bwj->bij/dot_general | solution.py:25
  257.2 0.0 copy-start.2
  257.2 0.0 all-reduce.3.cloned.1.call-update
  257.2 0.0 all-reduce.5.cloned.1.call-start
  257.3 17.1 %all-gather.10.cloned.1.call-done = bf16[512,4096]{1,0:T(8,128)(2,1)} async-done(((bf16[512,1024]{1,0:T(8,128)(2,1)}), bf16[512,4096]{1,0:T(8,128)(2,1)}) %all-gather.10.cloned.1.call-update) | async-done | bytes 4194320 | tf_op jit(solution)/shard_map/all_gather | solution.py:21
  274.3 0.0 copy-done.2
  274.3 8.9 convolution_convert_fusion
  283.3 0.0 all-reduce.5.cloned.1.call-update
  283.3 0.2 all-gather.8.cloned.1.call-start
  283.5 220.3 %all-gather.12.cloned.1.call-done = bf16[16,512,1024]{2,1,0:T(8,128)(2,1)} async-done(((bf16[2,512,1024]{2,1,0:T(8,128)(2,1)}), bf16[16,512,1024]{2,1,0:T(8,128)(2,1)}) %all-gather.12.cloned.1.call-update) | async-done | bytes 16777232 | tf_op jit(solution)/shard_map/all_gather | solution.py:8
  503.8 13.9 %copy.11 = bf16[2,8,512,1024]{3,2,1,0:T(8,128)(2,1)} copy(bf16[2,8,512,1024]{3,2,0,1:T(8,128)(2,1)} %bitcast.18) | data formatting | bytes 33554432 | tf_op jit(solution)/shard_map/reshape | solution.py:9
  517.7 139.4 %all-reduce.3.cloned.1.call-done = bf16[2,512,4096]{2,1,0:T(8,128)(2,1)} async-done(((bf16[2,512,4096]{2,1,0:T(8,128)(2,1)}), bf16[2,512,4096]{2,1,0:T(8,128)(2,1)}) %all-reduce.3.cloned.1.call-update) | async-done | bytes 8388624 | tf_op jit(solution)/shard_map/psum | solution.py:26
  657.2 15.7 %convolution_convert_fusion.2 = bf16[2,512,1024]{2,1,0:T(8,128)(2,1)} fusion(bf16[2,512,4096]{2,1,0:T(8,128)(2,1)} %all-reduce.3.cloned.1.call-done, bf16[2,4096,1024]{2,1,0:T(8,128)(2,1)} %bitcast.19), kind=kOutput, calls=%fused_computation.6 | convolution fusion | flops 8590983168 | bytes 27262976 | tf_op jit(solution)/shard_map/bij,bjk->bik/dot_general | solution.py:13
  672.9 0.0 all-gather.8.cloned.1.call-update
  672.9 258.2 %all-reduce.5.cloned.1.call-done = bf16[1024,4096]{1,0:T(8,128)(2,1)} async-done(((bf16[1024,4096]{1,0:T(8,128)(2,1)}), bf16[1024,4096]{1,0:T(8,128)(2,1)}) %all-reduce.5.cloned.1.call-update) | async-done | bytes 8388624 | tf_op jit(solution)/shard_map/psum | solution.py:23
  931.1 59.4 %all-gather.8.cloned.1.call-done = bf16[2,512,4096]{2,1,0:T(8,128)(2,1)} async-done(((bf16[2,512,1024]{2,1,0:T(8,128)(2,1)}), bf16[2,512,4096]{2,1,0:T(8,128)(2,1)}) %all-gather.8.cloned.1.call-update) | async-done | bytes 8388624 | tf_op jit(solution)/shard_map/all_gather | solution.py:29
  990.5 0.0 copy-start.1
  990.5 16.6 %divide_convert_fusion = (bf16[2,512,1024]{2,1,0:T(8,128)(2,1)}, bf16[2,512,1024]{2,1,0:T(8,128)(2,1)}) fusion(f32[2,512,1024]{2,1,0:T(8,128)} %param.7, bf16[2,512,4096]{2,1,0:T(8,128)(2,1)} %all-gather.8.cloned.1.call-done, bf16[1024,4096]{1,0:T(8,128)(2,1)} %all-reduce.5.cloned.1.call-done), kind=kOutput, calls=%fused_computation.4 | convolution fusion | flops 8595177472 | bytes 25165824 | tf_op jit(solution)/shard_map/bik,qk->biq/dot_general | solution.py:17
  1007.1 0.0 copy-done.1
Async XLA Ops:
  7.2 232.9 %copy-start = (bf16[2,1024,512]{2,1,0:T(8,128)(2,1)S(1)}, bf16[2,1024,512]{2,1,0:T(8,128)(2,1)}, u32[]{:S(2)}) copy-start(bf16[2,1024,512]{2,1,0:T(8,128)(2,1)} %param.9) | copy-start | bytes 6291460
  7.2 232.9 %all-gather.6.cloned.1.call-start = ((), (), s32[]{:S(2)}) async-start(), calls=%async_computation | async-start | bytes 18874368 | tf_op jit(solution)/shard_map/all_gather | solution.py:24
  7.9 266.4 %all-gather.10.cloned.1.call-start = ((), (), s32[]{:S(2)}) async-start(), calls=%async_computation.3 | async-start | bytes 5242880 | tf_op jit(solution)/shard_map/all_gather | solution.py:21
  8.7 495.1 %all-gather.12.cloned.1.call-start = ((), (), s32[]{:S(2)}) async-start(), calls=%async_computation.5 | async-start | bytes 18874368 | tf_op jit(solution)/shard_map/all_gather | solution.py:8
  9.4 647.8 %all-reduce.3.cloned.1.call-start = ((), (), s32[]{:S(2)}) async-start(), calls=%async_computation.1 | async-start | bytes 16777216 | tf_op jit(solution)/shard_map/psum | solution.py:26
  257.2 17.1 %copy-start.2 = (bf16[512,1024]{1,0:T(8,128)(2,1)S(1)}, bf16[512,1024]{1,0:T(8,128)(2,1)}, u32[]{:S(2)}) copy-start(bf16[512,1024]{1,0:T(8,128)(2,1)} %param.11) | copy-start | bytes 3145732
  257.2 673.9 %all-reduce.5.cloned.1.call-start = ((), (), s32[]{:S(2)}) async-start(), calls=%async_computation.4 | async-start | bytes 16777216 | tf_op jit(solution)/shard_map/psum | solution.py:23
  283.3 707.2 %all-gather.8.cloned.1.call-start = ((), (), s32[]{:S(2)}) async-start(), calls=%async_computation.2 | async-start | bytes 10485760 | tf_op jit(solution)/shard_map/all_gather | solution.py:29
  990.5 16.6 %copy-start.1 = (bf16[2,1024,512]{2,1,0:T(8,128)(2,1)S(1)}, bf16[2,1024,512]{2,1,0:T(8,128)(2,1)}, u32[]{:S(2)}) copy-start(bf16[2,1024,512]{2,1,0:T(8,128)(2,1)} %param.9) | copy-start | bytes 6291460
Sparse Core Ops, SparseCore 0:
  10.0 230.0 all-gather.5
  241.6 32.6 all-gather.9
  276.4 227.2 all-gather.11
  506.1 151.0 all-reduce.2
  660.9 270.1 all-reduce.4
  933.1 57.3 all-gather.7
